TPU v7x, 256 devices: a whole 4x4x8 slice. The times are simulated.
256 devices in a mesh: gx: 16 (over z, core), gy: 16 (over x, y).
Axes of the slice: x: 4, y: 4, z: 8, core: 2. Of those that a mesh axis runs over, the one named last changes fastest.
Arguments:
- tokens: bfloat16 [4096, 4096], P('gx', 'gy'), may hold values from -6 to 6
- gate_blocks: bfloat16 [16, 16, 10, 128, 128], P('gy', 'gx'), may hold values from -0.125 to 0.125
- up_blocks: bfloat16 [16, 16, 10, 128, 128], P('gy', 'gx'), may hold values from -0.125 to 0.125
- gate_coords: int32 [16, 16, 10, 2], P('gy', 'gx'), may hold values from 0 to 6, as said below
- gate_count: int32 [16, 16], P('gy', 'gx'), may hold values from 3 to 10, as said below
- down_blocks: bfloat16 [16, 16, 6, 128, 128], P('gx', 'gy'), may hold values from -0.09375 to 0.09375
- down_rows: int32 [16, 16, 4], P('gx'), may hold values from 0 to 6, as said below
- down_coords: int32 [16, 16, 6, 2], P('gx', 'gy'), may hold values from 0 to 3, as said below
- down_count: int32 [16, 16], P('gx', 'gy'), may hold values from 2 to 6, as said below
Outputs:
- mixed: bfloat16 [4096, 4096], P('gx', 'gy')
Inputs may be any that keep to these rules, and one draw needn't show every extreme that they name: `gate_coords`: within each tile the 10 (model-width block, hidden block) pairs are distinct, the first below 2, the second below 7; only the first gate_count slots are live. `gate_count`: some tile has all 10 slots live. `down_rows`: within each down tile the 4 hidden blocks are distinct. `down_coords`: within each down tile the 6 (kept-row index below 4, model-width block below 2) pairs are distinct; only the first down_count slots are live. `down_count`: some tile has all 6 slots live.
All inputs are finite; a program needn't handle non-finite values.
Results may differ from a plain program's by a relative error of at most 0.025.
Values may be sent and summed in bfloat16 or wider, within the bound.
A program may use at most 64 MiB of HBM per device.

v0:
```python
import jax
import jax.numpy as jnp
from jax import lax
from jax.sharding import PartitionSpec as P

FF = 14336
BLOCK = 128


def cut_along(value, dim, count):
    shape = value.shape
    parts = value.reshape(*shape[:dim], count, shape[dim] // count, *shape[dim + 1 :])
    return jnp.moveaxis(parts, dim, 0)


def piece_ends(length, count):
    hop = length // count
    if hop >= 8:
        hop -= hop % 8
    return [hop * k for k in range(1, count)]


def in_order(parts, dim):
    parts = jnp.moveaxis(parts, 0, dim)
    shape = parts.shape
    return parts.reshape(*shape[:dim], shape[dim] * shape[dim + 1], *shape[dim + 2 :])


def cut_exchange(value, axis, pieces, split_dim, concat_dim):
    parts = cut_along(value, split_dim, lax.axis_size(axis))
    split_at = max(range(1, max(2, parts.ndim - 1)), key=lambda d: parts.shape[d])
    done = []
    for section in jnp.split(parts, piece_ends(parts.shape[split_at], pieces), axis=split_at):
        if section.size:
            done.append(lax.all_to_all(section, axis, split_axis=0, concat_axis=0, tiled=True))
    return in_order(jnp.concatenate(done, axis=split_at), concat_dim)


def tile_dense(blocks, coords, count, row_count, col_count):
    live = (jnp.arange(coords.shape[0]) < count).astype(jnp.bfloat16)
    pick = jax.nn.one_hot(coords[:, 0], row_count, dtype=jnp.bfloat16)
    place = jax.nn.one_hot(coords[:, 1], col_count, dtype=jnp.bfloat16) * live[:, None]
    dense = jnp.einsum(
        "sr,sc,skm->rkcm", pick, place, blocks, preferred_element_type=jnp.float32
    ).astype(jnp.bfloat16)
    return dense.reshape(row_count * blocks.shape[1], col_count * blocks.shape[2])


def body(
    tokens,
    gate_blocks,
    up_blocks,
    gate_coords,
    gate_count,
    down_blocks,
    down_rows,
    down_coords,
    down_count,
):
    n_model = tokens.shape[1] // BLOCK
    n_hidden = FF // (BLOCK * lax.axis_size("gx"))
    paired_blocks = jnp.concatenate([gate_blocks[:, 0], up_blocks[:, 0]], -1)
    gathered = lax.all_gather(tokens, "gx", axis=0, tiled=True)
    tok_rows = gathered.shape[0] // lax.axis_size("gy")
    dense_pair = tile_dense(
        paired_blocks[0], gate_coords[0, 0], gate_count[0, 0], n_model, n_hidden
    )
    summed = lax.psum_scatter(
        jnp.dot(gathered, dense_pair, preferred_element_type=jnp.float32).astype(jnp.bfloat16),
        "gy",
        scatter_dimension=0,
        tiled=True,
    ).astype(jnp.float32)
    summed = summed.reshape(tok_rows, n_hidden, 2, BLOCK)
    hidden = (jax.nn.silu(summed[:, :, 0]) * summed[:, :, 1]).astype(jnp.bfloat16)
    kept_count = down_rows.shape[-1]
    dense_down = tile_dense(
        down_blocks[0, 0], down_coords[0, 0], down_count[0, 0], kept_count, n_model
    )
    select_every = jax.nn.one_hot(down_rows[0], n_hidden, dtype=jnp.bfloat16)
    outgoing = jnp.einsum(
        "nfk,guf->gnuk", hidden, select_every, preferred_element_type=jnp.float32
    ).astype(jnp.bfloat16)
    outgoing = outgoing.reshape(outgoing.shape[0], tok_rows, kept_count * BLOCK)
    received = cut_exchange(outgoing, "gy", 2, 0, 0)
    kept_all = received.reshape(received.shape[0] * tok_rows, kept_count * BLOCK)
    partial_out = jnp.dot(kept_all, dense_down, preferred_element_type=jnp.float32)
    return lax.psum_scatter(partial_out.astype(jnp.bfloat16), "gx", scatter_dimension=0, tiled=True)


def solution(mesh):
    return jax.shard_map(
        body,
        mesh=mesh,
        in_specs=(
            P("gx", "gy"),
            P("gy", "gx", None, None, None),
            P("gy", "gx", None, None, None),
            P("gy", "gx", None, None),
            P("gy", "gx"),
            P("gx", "gy", None, None, None),
            P("gx", None, None),
            P("gx", "gy", None, None),
            P("gx", "gy"),
        ),
        out_specs=P("gx", "gy"),
        check_vma=False,
    )
```

profile of v0, /device:TPU:2, one launch (start us, length us, event | category | flops | bytes accessed | tf_op | source)
XLA Modules:
  0.0 320.3 jit_solution(4454195248453779331)
XLA Ops:
  6.5 0.0 all-gather.2.cloned.1.call-start
  6.5 0.7 all-gather.2.cloned.1.call-update
  7.3 0.0 reduce-scatter.3.cloned.1.call-start
  8.0 0.8 slice_bitcast_fusion.5
  8.7 1.5 copy_bitcast_fusion
  10.3 0.4 convolution_convert_fusion.2
  10.7 0.3 copy.50
  11.0 40.6 %all-gather.2.cloned.1.call-done = bf16[4096,256]{1,0:T(8,128)(2,1)} async-done(((bf16[256,256]{1,0:T(8,128)(2,1)}), bf16[4096,256]{1,0:T(8,128)(2,1)}) %all-gather.2.cloned.1.call-update) | async-done | bytes 2097168 | tf_op jit(solution)/shard_map/all_gather | solution.py:63
  51.6 8.9 %fusion = bf16[4096,1792]{0,1:T(8,128)(2,1)} fusion(bf16[256,1792]{1,0:T(8,128)(2,1)S(1)} %bitcast.95, bf16[4096,256]{1,0:T(8,128)(2,1)} %all-gather.2.cloned.1.call-done), kind=kOutput, calls=%fused_computation.1 | convolution fusion | flops 3765436416 | bytes 17694720 | tf_op jit(solution)/shard_map/dot_general | solution.py:69
  60.5 0.0 reduce-scatter.3.cloned.1.call-update
  60.5 105.2 %reduce-scatter.3.cloned.1.call-done = bf16[256,1792]{0,1:T(8,128)(2,1)} async-done(((bf16[4096,1792]{0,1:T(8,128)(2,1)}), bf16[256,1792]{0,1:T(8,128)(2,1)}) %reduce-scatter.3.cloned.1.call-update) | async-done | bytes 917520 | tf_op jit(solution)/shard_map/reduce_scatter | solution.py:68
  165.7 1.3 fusion.31
  167.1 0.0 copy-start.1
  167.1 0.4 copy.48
  167.5 0.4 copy.49
  167.9 0.0 copy-done.1
  167.9 3.0 convert_bitcast_fusion
  170.9 7.5 %copy.37 = bf16[16,256,4,128]{1,3,2,0:T(8,128)(2,1)} copy(bf16[16,256,4,128]{3,0,1,2:T(8,128)(2,1)} %convert_bitcast_fusion) | data formatting | bytes 8388608 | tf_op jit(solution)/shard_map/convert_element_type | solution.py:83
  178.4 4.0 %slice_bitcast_fusion.1 = (bf16[16,1,128,512]{2,3,1,0:T(8,128)(2,1)S(1)}, bf16[16,1,128,512]{2,3,1,0:T(8,128)(2,1)}) fusion(bf16[16,1,256,512]{2,3,0,1:T(8,128)(2,1)} %bitcast.94), kind=kLoop, calls=%fused_computation.6 | loop fusion | bytes 8388608 | tf_op jit(solution)/shard_map/split | solution.py:33
  182.4 31.4 %all_to_all.10 = bf16[16,1,128,512]{2,3,1,0:T(8,128)(2,1)} all-to-all(bf16[16,1,128,512]{2,3,1,0:T(8,128)(2,1)S(1)} %get-tuple-element.5), channel_id=1, replica_groups=mesh['gx'=16,'gy'=16] {'gy'}, dimensions={0} | all-to-all | bytes 4194304 | tf_op jit(solution)/shard_map/all_to_all | solution.py:35
  213.8 0.0 copy-start.2
  213.8 0.0 copy-start
  213.8 6.0 %all-to-all-start.1 = ((bf16[16,1,128,512]{2,3,1,0:T(8,128)(2,1)}), bf16[16,1,128,512]{2,3,1,0:T(8,128)(2,1)S(1)}, u32[]{:S(2)}, u32[]{:S(2)}) async-start(bf16[16,1,128,512]{2,3,1,0:T(8,128)(2,1)} %get-tuple-element.6), calls=%async_computation.2 | async-start | bytes 4194304 | tf_op jit(solution)/shard_map/all_to_all | solution.py:35
  219.8 0.0 reduce-scatter.5.cloned.1.call-start
  220.5 0.0 copy-done.2
  220.5 0.0 copy-done
  220.5 0.2 fusion.1
  220.8 0.3 copy.43
  221.1 3.9 %copy.40 = bf16[16,1,128,512]{3,2,0,1:T(8,128)(2,1)} copy(bf16[16,1,128,512]{2,3,1,0:T(8,128)(2,1)} %all_to_all.10) | data formatting | bytes 4194304 | tf_op jit(solution)/shard_map/all_to_all | solution.py:35
  225.0 20.5 %all-to-all-done.1 = bf16[16,1,128,512]{2,3,1,0:T(8,128)(2,1)S(1)} async-done(((bf16[16,1,128,512]{2,3,1,0:T(8,128)(2,1)}), bf16[16,1,128,512]{2,3,1,0:T(8,128)(2,1)S(1)}, u32[]{:S(2)}, u32[]{:S(2)}) %all-to-all-start.1) | async-done | bytes 2097184 | tf_op jit(solution)/shard_map/all_to_all | solution.py:35
  245.4 2.6 copy.41
  248.0 2.6 pad_maximum_fusion
  250.6 2.6 convolution_convert_fusion.1
  253.2 0.0 reduce-scatter.5.cloned.1.call-update
  253.2 60.6 %reduce-scatter.5.cloned.1.call-done = bf16[256,256]{1,0:T(8,128)(2,1)} async-done(((bf16[4096,256]{1,0:T(8,128)(2,1)}), bf16[256,256]{1,0:T(8,128)(2,1)}) %reduce-scatter.5.cloned.1.call-update) | async-done | bytes 131088 | tf_op jit(solution)/shard_map/reduce_scatter | solution.py:88
  (7 shorter events, 0.0 us)
Async XLA Ops:
  6.5 45.1 %all-gather.2.cloned.1.call-start = ((), (), s32[]{:S(2)}) async-start(), calls=%async_computation.4 | async-start | bytes 2228224 | tf_op jit(solution)/shard_map/all_gather | solution.py:63
  7.3 158.5 %reduce-scatter.3.cloned.1.call-start = ((), (), s32[]{:S(2)}) async-start(), calls=%async_computation.5 | async-start | bytes 15597568 | tf_op jit(solution)/shard_map/reduce_scatter | solution.py:68
  167.1 0.8 copy-start.1
  213.8 6.7 %copy-start.2 = (s32[1,1,6,2]{2,3,1,0:T(2,128)S(1)}, s32[1,1,6,2]{2,3,1,0:T(2,128)}, u32[]{:S(2)}) copy-start(s32[1,1,6,2]{2,3,1,0:T(2,128)} %param.16) | copy-start | bytes 148
  213.8 6.7 %copy-start = (bf16[1,1,6,128,128]{4,3,2,1,0:T(8,128)(2,1)S(1)}, bf16[1,1,6,128,128]{4,3,2,1,0:T(8,128)(2,1)}, u32[]{:S(2)}) copy-start(bf16[1,1,6,128,128]{4,3,2,1,0:T(8,128)(2,1)} %param.14) | copy-start | bytes 589828
  213.8 31.6 %all-to-all-start.1 = ((bf16[16,1,128,512]{2,3,1,0:T(8,128)(2,1)}), bf16[16,1,128,512]{2,3,1,0:T(8,128)(2,1)S(1)}, u32[]{:S(2)}, u32[]{:S(2)}) async-start(bf16[16,1,128,512]{2,3,1,0:T(8,128)(2,1)} %get-tuple-element.6), calls=%async_computation.2 | async-start | bytes 4194304 | tf_op jit(solution)/shard_map/all_to_all | solution.py:35
  219.8 94.0 %reduce-scatter.5.cloned.1.call-start = ((), (), s32[]{:S(2)}) async-start(), calls=%async_computation.6 | async-start | bytes 2228224 | tf_op jit(solution)/shard_map/reduce_scatter | solution.py:88
Sparse Core Ops, SparseCore 0:
  9.2 42.3 all-gather.1
  60.6 105.0 reduce-scatter.2
  253.3 60.4 reduce-scatter.4
where the time goes:
time: 321 us; the launch traced here: 320 us
  waiting for transfers between devices  228 us (71%)
  blocking collectives  31.4 us (10%)
  local copies, waits for them, and re-layouts  23 us (7%)
  matrix products  15.1 us (5%)
  between operations  14.5 us (5%)
  starting transfers between devices  6.04 us (2%)
    reduce_scatter x1, waiting for transfers between devices, body(): lax.psum_scatter(jnp.dot(gathered, dense_pair, preferred_element_type=jnp...  105 us
    reduce_scatter x1, waiting for transfers between devices, body(): lax.psum_scatter(partial_out.astype(jnp.bfloat16), 'gx', scatter_dimensio...  60.6 us
    all_gather x1, waiting for transfers between devices, body(): gathered = lax.all_gather(tokens, 'gx', axis=0, tiled=True)  40.6 us
    all_to_all x1, blocking collectives, cut_exchange(): lax.all_to_all(section, axis, split_axis=0, concat_axis=0, tiled=True)  31.4 us
    all_to_all x1, waiting for transfers between devices, cut_exchange(): lax.all_to_all(section, axis, split_axis=0, concat_axis=0, tiled=True)  20.5 us
    dot_general x1, matrix products, body(): jnp.dot(gathered, dense_pair, preferred_element_type=jnp.float32)  8.91 us
    convert_element_type x1, local copies, waits for them, and re-layouts, body(): outgoing = jnp.einsum('nfk,guf->gnuk', hidden, select_every, preferred_el...  7.47 us
    all_to_all x2, local copies, waits for them, and re-layouts, cut_exchange(): lax.all_to_all(section, axis, split_axis=0, concat_axis=0, tiled=True)  6.51 us
  transfers between devices with their start and end apart: 4, of which 4 were waited for; matrix products, arithmetic and copies ran while one was open for 2% of the time, Pallas kernels for 0%

commit v1 on v0

--- a/solution.py
+++ b/solution.py
@@ -5,6 +5,18 @@
 
 FF = 14336
 BLOCK = 128
+
+
+def gather_by_bits(shard, axis, dim):
+    ways, here, step = (lax.axis_size(axis), lax.axis_index(axis), shard.shape[dim])
+    line, have = (shard, 1)
+    while have < ways:
+        line = jnp.concatenate(
+            [line, lax.ppermute(line, axis, [(d, (d - have) % ways) for d in range(ways)])],
+            axis=dim,
+        )
+        have = 2 * have
+    return jnp.roll(line, here * step, axis=dim)
 
 
 def cut_along(value, dim, count):
@@ -60,7 +72,7 @@
     n_model = tokens.shape[1] // BLOCK
     n_hidden = FF // (BLOCK * lax.axis_size("gx"))
     paired_blocks = jnp.concatenate([gate_blocks[:, 0], up_blocks[:, 0]], -1)
-    gathered = lax.all_gather(tokens, "gx", axis=0, tiled=True)
+    gathered = gather_by_bits(tokens, "gx", 0)
     tok_rows = gathered.shape[0] // lax.axis_size("gy")
     dense_pair = tile_dense(
         paired_blocks[0], gate_coords[0, 0], gate_count[0, 0], n_model, n_hidden

time: 321 us -> 378 us (1.18)
  waiting for transfers between devices: 228 us -> 263 us
  starting transfers between devices: 6.04 us -> 19.4 us
  other arithmetic: 2.61 us -> 6.42 us
  local copies, waits for them, and re-layouts: 23 us -> 26.8 us
    ppermute x0 -> x4, waiting for transfers between devices: none -> 73.6 us  [gather_by_bits(): lax.ppermute(line, axis, [(d, (d - have) % ways) for d in range(ways)])]
    all_gather x1 -> x0, waiting for transfers between devices: 40.6 us -> none  [body(): gathered = lax.all_gather(tokens, 'gx', axis=0, tiled=True)]
    ppermute x0 -> x4, starting transfers between devices: none -> 13.3 us  [gather_by_bits(): lax.ppermute(line, axis, [(d, (d - have) % ways) for d in range(ways)])]
    concatenate x0 -> x3, other arithmetic: none -> 3.81 us  [gather_by_bits(): jnp.concatenate([line, lax.ppermute(line, axis, [(d, (d - have) % ways) f...]
  transfers between devices with their start and end apart: 4 -> 7, of which waited for: 4 -> 7; matrix products, arithmetic and copies ran while one was open for 2% -> 2% of each run, Pallas kernels for 0% -> 0%
where the time goes in v1:
time: 378 us; the launch traced here: 377 us
  waiting for transfers between devices  263 us (70%)
  blocking collectives  31.6 us (8%)
  local copies, waits for them, and re-layouts  26.8 us (7%)
  starting transfers between devices  19.4 us (5%)
  matrix products  15.6 us (4%)
  between operations  14.9 us (4%)
  other arithmetic  6.42 us (2%)
    reduce_scatter x1, waiting for transfers between devices, body(): lax.psum_scatter(jnp.dot(gathered, dense_pair, preferred_element_type=jnp...  108 us
    ppermute x4, waiting for transfers between devices, gather_by_bits(): lax.ppermute(line, axis, [(d, (d - have) % ways) for d in range(ways)])  73.6 us
    reduce_scatter x1, waiting for transfers between devices, body(): lax.psum_scatter(partial_out.astype(jnp.bfloat16), 'gx', scatter_dimensio...  60.4 us
    all_to_all x1, blocking collectives, cut_exchange(): lax.all_to_all(section, axis, split_axis=0, concat_axis=0, tiled=True)  31.6 us
    all_to_all x1, waiting for transfers between devices, cut_exchange(): lax.all_to_all(section, axis, split_axis=0, concat_axis=0, tiled=True)  20.4 us
    ppermute x4, starting transfers between devices, gather_by_bits(): lax.ppermute(line, axis, [(d, (d - have) % ways) for d in range(ways)])  13.3 us
    dot_general x1, matrix products, body(): jnp.dot(gathered, dense_pair, preferred_element_type=jnp.float32)  9.32 us
  transfers between devices with their start and end apart: 7, of which 7 were waited for; matrix products, arithmetic and copies ran while one was open for 2% of the time, Pallas kernels for 0%

profile of v1, /device:TPU:2, one launch (start us, length us, event | category | flops | bytes accessed | tf_op | source)
XLA Modules:
  0.0 377.3 jit_solution(14268128567473515918)
XLA Ops:
  6.5 0.0 reduce-scatter.3.cloned.1.call-start
  6.5 5.3 %collective-permute-start = (bf16[256,256]{1,0:T(8,128)(2,1)}, bf16[256,256]{1,0:T(8,128)(2,1)S(1)}, u32[]{:S(2)}, u32[]{:S(2)}) collective-permute-start(bf16[256,256]{1,0:T(8,128)(2,1)} %param.9), channel_id=1, source_target_pairs={{0,240},{16,0},{32,16},{48,32},{64,48},{80,64},{96,80},{112,96},{1... | collective-permute-start | bytes 393224 | tf_op jit(solution)/shard_map/ppermute | solution.py:15
  11.8 2.8 collective-permute-done
  14.7 0.9 pad_maximum_fusion.3
  15.6 1.1 collective-permute-start.1
  17.3 4.7 %collective-permute-done.1 = bf16[512,256]{1,0:T(8,128)(2,1)S(1)} collective-permute-done((bf16[512,256]{1,0:T(8,128)(2,1)S(1)}, bf16[512,256]{1,0:T(8,128)(2,1)S(1)}, u32[]{:S(2)}, u32[]{:S(2)}) %collective-permute-start.1) | collective-permute-done | bytes 262176 | tf_op jit(solution)/shard_map/ppermute | solution.py:15
  22.0 0.9 pad_maximum_fusion.2
  23.0 0.0 copy-start
  23.0 3.7 collective-permute-start.2
  26.7 0.8 slice_bitcast_fusion.5
  27.4 19.7 %collective-permute-done.2 = bf16[1024,256]{1,0:T(8,128)(2,1)S(1)} collective-permute-done((bf16[1024,256]{1,0:T(8,128)(2,1)S(1)}, bf16[1024,256]{1,0:T(8,128)(2,1)S(1)}, u32[]{:S(2)}, u32[]{:S(2)}) %collective-permute-start.2) | collective-permute-done | bytes 524320 | tf_op jit(solution)/shard_map/ppermute | solution.py:15
  47.1 1.9 pad_maximum_fusion.1
  49.1 3.3 collective-permute-start.3
  52.4 1.5 copy_bitcast_fusion.2
  53.9 0.4 convolution_convert_fusion.2
  54.4 0.3 copy.50
  54.6 0.0 copy-done
  54.8 46.4 %collective-permute-done.3 = bf16[2048,256]{1,0:T(8,128)(2,1)S(1)} collective-permute-done((bf16[2048,256]{1,0:T(8,128)(2,1)}, bf16[2048,256]{1,0:T(8,128)(2,1)S(1)}, u32[]{:S(2)}, u32[]{:S(2)}) %collective-permute-start.3) | collective-permute-done | bytes 1048608 | tf_op jit(solution)/shard_map/ppermute | solution.py:15
  101.1 0.1 constant_dynamic-update-slice_fusion.5
  101.3 0.1 constant_dynamic-update-slice_fusion
  101.4 0.0 copy-start.1
  101.4 1.9 copy-done.1
  103.3 9.3 %convolution_convert_fusion = bf16[4096,1792]{1,0:T(8,128)(2,1)} fusion(bf16[256,1792]{1,0:T(8,128)(2,1)S(1)} %bitcast.97, bf16[8192,256]{1,0:T(8,128)(2,1)} %copy-done.1, s32[]{:T(128)S(6)} %select_n.14), kind=kOutput, calls=%fused_computation | convolution fusion | flops 3765436416 | bytes 17694724 | tf_op jit(solution)/shard_map/dot_general | solution.py:81
  112.7 0.0 reduce-scatter.3.cloned.1.call-update
  112.7 0.0 copy-start.3
  112.7 108.2 %reduce-scatter.3.cloned.1.call-done = bf16[256,1792]{1,0:T(8,128)(2,1)} async-done(((bf16[4096,1792]{1,0:T(8,128)(2,1)}), bf16[256,1792]{1,0:T(8,128)(2,1)}) %reduce-scatter.3.cloned.1.call-update) | async-done | bytes 917520 | tf_op jit(solution)/shard_map/reduce_scatter | solution.py:80
  220.9 2.2 reshape.29
  223.1 1.4 fusion.35
  224.5 0.0 copy-done.3
  224.5 3.0 convert_bitcast_fusion
  227.5 7.5 %copy.37 = bf16[16,256,4,128]{1,3,2,0:T(8,128)(2,1)} copy(bf16[16,256,4,128]{3,0,1,2:T(8,128)(2,1)} %convert_bitcast_fusion) | data formatting | bytes 8388608 | tf_op jit(solution)/shard_map/convert_element_type | solution.py:95
  235.0 4.0 %slice_bitcast_fusion.1 = (bf16[16,1,128,512]{2,3,1,0:T(8,128)(2,1)S(1)}, bf16[16,1,128,512]{2,3,1,0:T(8,128)(2,1)}) fusion(bf16[16,1,256,512]{2,3,0,1:T(8,128)(2,1)} %bitcast.94), kind=kLoop, calls=%fused_computation.5 | loop fusion | bytes 8388608 | tf_op jit(solution)/shard_map/split | solution.py:45
  239.0 0.0 copy-start.4
  239.0 0.0 copy-start.2
  239.0 31.6 %all_to_all.10 = bf16[16,1,128,512]{2,3,1,0:T(8,128)(2,1)} all-to-all(bf16[16,1,128,512]{2,3,1,0:T(8,128)(2,1)S(1)} %get-tuple-element.5), channel_id=1, replica_groups=mesh['gx'=16,'gy'=16] {'gy'}, dimensions={0} | all-to-all | bytes 4194304 | tf_op jit(solution)/shard_map/all_to_all | solution.py:47
  270.6 5.8 %all-to-all-start.1 = ((bf16[16,1,128,512]{2,3,1,0:T(8,128)(2,1)}), bf16[16,1,128,512]{2,3,1,0:T(8,128)(2,1)S(1)}, u32[]{:S(2)}, u32[]{:S(2)}) async-start(bf16[16,1,128,512]{2,3,1,0:T(8,128)(2,1)} %get-tuple-element.6), calls=%async_computation.2 | async-start | bytes 4194304 | tf_op jit(solution)/shard_map/all_to_all | solution.py:47
  276.4 0.2 reduce-scatter.5.cloned.1.call-start
  277.3 0.0 copy-done.4
  277.4 0.0 copy-done.2
  277.4 0.2 fusion.1
  277.6 0.3 copy.43
  277.9 3.9 %copy.40 = bf16[16,1,128,512]{3,2,0,1:T(8,128)(2,1)} copy(bf16[16,1,128,512]{2,3,1,0:T(8,128)(2,1)} %all_to_all.10) | data formatting | bytes 4194304 | tf_op jit(solution)/shard_map/all_to_all | solution.py:47
  281.9 20.4 %all-to-all-done.1 = bf16[16,1,128,512]{2,3,1,0:T(8,128)(2,1)S(1)} async-done(((bf16[16,1,128,512]{2,3,1,0:T(8,128)(2,1)}), bf16[16,1,128,512]{2,3,1,0:T(8,128)(2,1)S(1)}, u32[]{:S(2)}, u32[]{:S(2)}) %all-to-all-start.1) | async-done | bytes 2097184 | tf_op jit(solution)/shard_map/all_to_all | solution.py:47
  302.2 2.6 copy.41
  304.8 2.6 pad_maximum_fusion
  307.4 2.6 convolution_convert_fusion.1
  310.0 0.0 reduce-scatter.5.cloned.1.call-update
  310.0 60.4 %reduce-scatter.5.cloned.1.call-done = bf16[256,256]{1,0:T(8,128)(2,1)} async-done(((bf16[4096,256]{1,0:T(8,128)(2,1)}), bf16[256,256]{1,0:T(8,128)(2,1)}) %reduce-scatter.5.cloned.1.call-update) | async-done | bytes 131088 | tf_op jit(solution)/shard_map/reduce_scatter | solution.py:100
  (15 shorter events, 0.2 us)
Async XLA Ops:
  6.5 214.4 %reduce-scatter.3.cloned.1.call-start = ((), (), s32[]{:S(2)}) async-start(), calls=%async_computation.4 | async-start | bytes 15597568 | tf_op jit(solution)/shard_map/reduce_scatter | solution.py:80
  6.5 8.1 %collective-permute-start = (bf16[256,256]{1,0:T(8,128)(2,1)}, bf16[256,256]{1,0:T(8,128)(2,1)S(1)}, u32[]{:S(2)}, u32[]{:S(2)}) collective-permute-start(bf16[256,256]{1,0:T(8,128)(2,1)} %param.9), channel_id=1, source_target_pairs={{0,240},{16,0},{32,16},{48,32},{64,48},{80,64},{96,80},{112,96},{1... | collective-permute-start | bytes 393224 | tf_op jit(solution)/shard_map/ppermute | solution.py:15
  15.6 6.5 %collective-permute-start.1 = (bf16[512,256]{1,0:T(8,128)(2,1)S(1)}, bf16[512,256]{1,0:T(8,128)(2,1)S(1)}, u32[]{:S(2)}, u32[]{:S(2)}) collective-permute-start(bf16[512,256]{1,0:T(8,128)(2,1)S(1)} %pad_maximum_fusion.3), channel_id=1, source_target_pairs={{0,224},{16,240},{32,0},{48,16},{64,32},{80,48},{96,64},{112,80},{... | collective-permute-start | bytes 786440 | tf_op jit(solution)/shard_map/ppermute | solution.py:15
  23.0 31.6 %copy-start = (bf16[256,256]{1,0:T(8,128)(2,1)S(1)}, bf16[256,256]{1,0:T(8,128)(2,1)}, u32[]{:S(2)}) copy-start(bf16[256,256]{1,0:T(8,128)(2,1)} %param.9) | copy-start | bytes 393220
  23.0 24.1 %collective-permute-start.2 = (bf16[1024,256]{1,0:T(8,128)(2,1)S(1)}, bf16[1024,256]{1,0:T(8,128)(2,1)S(1)}, u32[]{:S(2)}, u32[]{:S(2)}) collective-permute-start(bf16[1024,256]{1,0:T(8,128)(2,1)S(1)} %pad_maximum_fusion.2), channel_id=1, source_target_pairs={{0,192},{16,208},{32,224},{48,240},{64,0},{80,16},{96,32},{112,48}... | collective-permute-start | bytes 1572872 | tf_op jit(solution)/shard_map/ppermute | solution.py:15
  49.1 52.0 %collective-permute-start.3 = (bf16[2048,256]{1,0:T(8,128)(2,1)}, bf16[2048,256]{1,0:T(8,128)(2,1)S(1)}, u32[]{:S(2)}, u32[]{:S(2)}) collective-permute-start(bf16[2048,256]{1,0:T(8,128)(2,1)} %pad_maximum_fusion.1), channel_id=1, source_target_pairs={{0,128},{16,144},{32,160},{48,176},{64,192},{80,208},{96,224},{112... | collective-permute-start | bytes 3145736 | tf_op jit(solution)/shard_map/ppermute | solution.py:15
  101.4 2.0 copy-start.1
  112.7 111.8 %copy-start.3 = (s32[1,16,4]{1,2,0:T(4,128)S(1)}, s32[1,16,4]{1,2,0:T(4,128)}, u32[]{:S(2)}) copy-start(s32[1,16,4]{1,2,0:T(4,128)} %param.15) | copy-start | bytes 772
  239.0 38.3 %copy-start.4 = (s32[1,1,6,2]{2,3,1,0:T(2,128)S(1)}, s32[1,1,6,2]{2,3,1,0:T(2,128)}, u32[]{:S(2)}) copy-start(s32[1,1,6,2]{2,3,1,0:T(2,128)} %param.16) | copy-start | bytes 148
  239.0 38.4 %copy-start.2 = (bf16[1,1,6,128,128]{4,3,2,1,0:T(8,128)(2,1)S(1)}, bf16[1,1,6,128,128]{4,3,2,1,0:T(8,128)(2,1)}, u32[]{:S(2)}) copy-start(bf16[1,1,6,128,128]{4,3,2,1,0:T(8,128)(2,1)} %param.14) | copy-start | bytes 589828
  270.6 31.6 %all-to-all-start.1 = ((bf16[16,1,128,512]{2,3,1,0:T(8,128)(2,1)}), bf16[16,1,128,512]{2,3,1,0:T(8,128)(2,1)S(1)}, u32[]{:S(2)}, u32[]{:S(2)}) async-start(bf16[16,1,128,512]{2,3,1,0:T(8,128)(2,1)} %get-tuple-element.6), calls=%async_computation.2 | async-start | bytes 4194304 | tf_op jit(solution)/shard_map/all_to_all | solution.py:47
  276.4 94.0 %reduce-scatter.5.cloned.1.call-start = ((), (), s32[]{:S(2)}) async-start(), calls=%async_computation.5 | async-start | bytes 2228224 | tf_op jit(solution)/shard_map/reduce_scatter | solution.py:100
Sparse Core Ops, SparseCore 0:
  112.8 108.0 reduce-scatter.2
  310.2 60.2 reduce-scatter.4
